TPU v7x, 32 devices: a whole 2x2x4 slice. The times are simulated.
32 devices in a mesh: dp: 8 (over z, y), mp: 4 (over x, core).
Axes of the slice: x: 2, y: 2, z: 4, core: 2. Of those that a mesh axis runs over, the one named last changes fastest.
Arguments:
- tokens: bfloat16 [49152, 512], P('dp'), may hold values from -6 to 6
- w_uvqk: bfloat16 [512, 2048], P(None, 'mp')
- w_out: bfloat16 [512, 512], replicated, may hold values from -0.25 to 0.25
- hist_len: int32 [8, 24], P('dp'), may hold values from 64 to 256, as said below
- owner: int32 [8, 24], P('dp'), may hold values from 0 to 7, as said below
- recv_offset: int32 [8, 24], P('dp'), may hold values from 0 to 47, as said below
- block_start: int32 [8, 24], P('dp'), may hold values from 0 to 47, as said below
Outputs:
- packed_out: bfloat16 [49152, 512], P('dp', 'mp')
- user_state: bfloat16 [192, 512], P('dp', 'mp')
Inputs may be any that keep to these rules, and one draw needn't show every extreme that they name: User (d, u) has ceil(hist_len / 128) blocks, at most 2. owner[d, u] = (p(d) + r(u mod 8)) mod 8 for two permutations p, r of the indices of dp drawn from the seed: every owner receives exactly 24 users, and one device sends at most 3 users to one owner. On some owner every received user has 2 blocks. `recv_offset`: the users of one owner occupy disjoint runs of its 48 blocks, in the order of u; on some owner they fill all 48 blocks. `block_start`: the users of one device occupy disjoint runs of its 48 blocks, in the order of u.
All inputs are finite; a program needn't handle non-finite values.
Results may differ from a plain program's by a relative error of at most 0.0059.
Values may be sent and summed in bfloat16 or wider, within the bound.
A program may use at most 128 MiB of HBM per device.

v0:
```python
import jax
import jax.numpy as jnp
from jax import lax
from jax.sharding import PartitionSpec as P

D = 512
HEADS = 4
BLOCK = 128
MAXB = 2
BLK_DEV = 48


EPS = 1e-05


def norm_rows(values):
    average = jnp.mean(values, axis=-1, keepdims=True)
    variance = jnp.mean(values * values, axis=-1, keepdims=True) - average * average
    return (values - average) * lax.rsqrt(variance + EPS)


def attend(query, keys, values, query_user, key_user):
    row_count, head_size = query.shape
    tile_rows = 4 * BLOCK
    back_rows = (MAXB - 1) * BLOCK
    scaling = (D // HEADS) ** (-0.5)
    keys_ext = jnp.concatenate([jnp.zeros((back_rows, head_size), keys.dtype), keys], 0)
    values_ext = jnp.concatenate([jnp.zeros((back_rows, head_size), values.dtype), values], 0)
    users_ext = jnp.concatenate([jnp.full((back_rows,), -2, jnp.int32), key_user], 0)
    query_pos = jnp.arange(tile_rows, dtype=jnp.int32)[:, None] + back_rows
    key_pos = jnp.arange(tile_rows + back_rows, dtype=jnp.int32)[None, :]

    def one_tile(start):
        query_tile = lax.dynamic_slice_in_dim(query, start, tile_rows, 0)
        key_tile = lax.dynamic_slice_in_dim(keys_ext, start, tile_rows + back_rows, 0)
        value_tile = lax.dynamic_slice_in_dim(values_ext, start, tile_rows + back_rows, 0)
        query_owner = lax.dynamic_slice_in_dim(query_user, start, tile_rows, 0)
        key_owner = lax.dynamic_slice_in_dim(users_ext, start, tile_rows + back_rows, 0)
        raw_scores = (
            lax.dot_general(
                query_tile, key_tile, (((1,), (1,)), ((), ())), preferred_element_type=jnp.float32
            )
            * scaling
        )
        allowed = (query_owner[:, None] == key_owner[None, :]) & (key_pos <= query_pos)
        weights = jnp.where(allowed, jax.nn.silu(raw_scores) / (MAXB * BLOCK), 0.0).astype(
            jnp.bfloat16
        )
        return jnp.dot(weights, value_tile, preferred_element_type=jnp.float32)

    tile_starts = jnp.arange(row_count // tile_rows, dtype=jnp.int32) * tile_rows
    return lax.map(one_tile, tile_starts).reshape(row_count, head_size)


def layer_rows(rows_in, query_user, key_user, w_uvqk, w_out):
    row_count = rows_in.shape[0]
    head_size = D // HEADS
    mp_size = lax.axis_size("mp")
    portion = lax.axis_index("mp")
    quarter = D // mp_size
    local_heads = w_uvqk.shape[1] // (4 * head_size)
    widened = rows_in.astype(jnp.float32)
    normed = norm_rows(widened).astype(jnp.bfloat16)
    projected = jax.nn.silu(jnp.dot(normed, w_uvqk, preferred_element_type=jnp.float32)).astype(
        jnp.bfloat16
    )
    pieces = projected.reshape(row_count, local_heads, 4, head_size)
    outputs = attend(pieces[:, 0, 2], pieces[:, 0, 3], pieces[:, 0, 1], query_user, key_user)
    totals = lax.psum((jnp.sum(outputs, 1), jnp.sum(outputs * outputs, 1)), "mp")
    average = totals[0] / D
    variance = totals[1] / D - average * average
    gates = pieces[:, :, 0].reshape(row_count, local_heads * head_size).astype(jnp.float32)
    gated_rows = ((outputs - average[:, None]) * lax.rsqrt(variance + EPS)[:, None] * gates).astype(
        jnp.bfloat16
    )
    own_rows = lax.dynamic_slice_in_dim(
        w_out, portion * local_heads * head_size, local_heads * head_size, 0
    )
    partial_term = jnp.dot(gated_rows, own_rows, preferred_element_type=jnp.float32)
    mixed_rows = lax.psum_scatter(partial_term, "mp", scatter_dimension=1, tiled=True)
    residual = lax.dynamic_slice_in_dim(widened, portion * quarter, quarter, 1)
    return (mixed_rows + residual).astype(jnp.bfloat16)


def row_labels(block_user, block_fill):
    in_block = jnp.arange(BLOCK, dtype=jnp.int32)[None, :]
    row_live = (in_block < block_fill[:, None]).reshape(-1)
    row_user = jnp.broadcast_to(block_user[:, None], (block_user.shape[0], BLOCK)).reshape(-1)
    return (row_live, jnp.where(row_live, row_user, -3), jnp.where(row_live, row_user, -2))


def per_device(tokens, w_uvqk, w_out, hist_len, owner, recv_offset, block_start):
    dp_size = lax.axis_size("dp")
    mp_size = lax.axis_size("mp")
    myself = lax.axis_index("dp")
    user_count = hist_len.shape[1]
    per_pair = -(-user_count // dp_size)
    pair_cap = per_pair * MAXB
    quarter = D // mp_size
    lengths = hist_len[0]
    owners = owner[0]
    starts = block_start[0]
    counts = (lengths + BLOCK - 1) // BLOCK
    user_ids = jnp.arange(user_count, dtype=jnp.int32)
    earlier = user_ids[None, :] < user_ids[:, None]
    same_owner = (owners[:, None] == owners[None, :]) & earlier
    in_pair = jnp.sum(jnp.where(same_owner, counts[None, :], 0), axis=1)
    slot_ids = jnp.arange(pair_cap, dtype=jnp.int32)
    device_ids = jnp.arange(dp_size, dtype=jnp.int32)
    slot_step = slot_ids[None, :, None] - in_pair[None, None, :]
    sending = (
        (owners[None, None, :] == device_ids[:, None, None])
        & (slot_step >= 0)
        & (slot_step < counts[None, None, :])
    )
    send_block = jnp.sum(jnp.where(sending, starts[None, None, :] + slot_step, 0), axis=2)
    all_len, all_owner, all_offset = (
        lax.all_gather(hist_len, "dp", axis=0, tiled=True),
        lax.all_gather(owner, "dp", axis=0, tiled=True),
        lax.all_gather(recv_offset, "dp", axis=0, tiled=True),
    )
    all_counts = (all_len + BLOCK - 1) // BLOCK
    all_before = (all_owner[:, :, None] == all_owner[:, None, :]) & earlier[None]
    all_in_pair = jnp.sum(jnp.where(all_before, all_counts[:, None, :], 0), axis=2)
    owned = all_owner == myself
    flat_owned = owned.reshape(-1)
    flat_len = all_len.reshape(-1)
    flat_offset = all_offset.reshape(-1)
    flat_counts = all_counts.reshape(-1)
    flat_in_pair = all_in_pair.reshape(-1)
    candidate_ids = jnp.arange(dp_size * user_count, dtype=jnp.int32)
    source_ids = candidate_ids // user_count
    block_ids = jnp.arange(BLK_DEV, dtype=jnp.int32)
    land_step = block_ids[:, None] - flat_offset[None, :]
    landed = flat_owned[None, :] & (land_step >= 0) & (land_step < flat_counts[None, :])
    slot_index = jnp.sum(
        jnp.where(landed, source_ids[None, :] * pair_cap + flat_in_pair[None, :] + land_step, 0),
        axis=1,
    )
    owned_user = jnp.sum(jnp.where(landed, candidate_ids[None, :], 0), axis=1)
    owned_fill = jnp.sum(
        jnp.where(landed, jnp.clip(flat_len[None, :] - land_step * BLOCK, 0, BLOCK), 0), axis=1
    )
    owned_live, owned_query, owned_key = row_labels(owned_user, owned_fill)
    local_step = block_ids[:, None] - starts[None, :]
    within = (local_step >= 0) & (local_step < counts[None, :])
    local_user = jnp.sum(jnp.where(within, user_ids[None, :], 0), axis=1)
    local_fill = jnp.sum(
        jnp.where(within, jnp.clip(lengths[None, :] - local_step * BLOCK, 0, BLOCK), 0), axis=1
    )
    local_live, local_query, local_key = row_labels(local_user, local_fill)
    results = layer_rows(tokens, local_query, local_key, w_uvqk, w_out)
    state = jnp.take(results, starts * BLOCK + lengths - 1, axis=0)
    outgoing = jnp.take(results.reshape(BLK_DEV, BLOCK, quarter), send_block, axis=0)
    arrived = lax.all_to_all(outgoing, "dp", split_axis=0, concat_axis=0, tiled=True)
    gathered = jnp.take(
        arrived.reshape(dp_size * pair_cap, BLOCK, quarter), slot_index, axis=0
    ).reshape(BLK_DEV * BLOCK, quarter)
    packed = jnp.where(owned_live[:, None], gathered, jnp.zeros_like(gathered))
    return (packed, state)


def solution(mesh):
    in_specs = (
        P("dp", None),
        P(None, "mp"),
        P(),
        P("dp", None),
        P("dp", None),
        P("dp", None),
        P("dp", None),
    )
    out_specs = (P("dp", "mp"), P("dp", "mp"))
    return jax.shard_map(
        per_device, mesh=mesh, in_specs=in_specs, out_specs=out_specs, check_vma=False
    )
```

profile of v0, /device:TPU:0, one launch (start us, length us, event | category | flops | bytes accessed | tf_op | source)
XLA Modules:
  0.0 330.3 jit_solution(3480145487422922043)
XLA Ops:
  7.3 4.8 %convert_reduce_fusion = (f32[6144]{0:T(1024)S(1)}, f32[6144]{0:T(1024)S(1)}) fusion(bf16[6144,512]{1,0:T(8,128)(2,1)} %param.9), kind=kLoop, calls=%fused_computation.31 | loop fusion | flops 12570624 | bytes 6340608 | tf_op jit(solution)/shard_map/reduce_sum | solution.py:17
  12.1 8.0 %multiply_convert_fusion = bf16[6144,512]{0,1:T(8,128)(2,1)S(1)} fusion(bf16[512,512]{1,0:T(8,128)(2,1)S(1)} %copy-done, bf16[6144,512]{1,0:T(8,128)(2,1)S(1)} %copy-done.2, f32[6144]{0:T(1024)S(1)} %get-tuple-element.106, f32[6144]{0:T(1024)S(1)} %get-tuple-element.105), kind=kOutput, calls=%fused_computation.28 | convolution fusion | flops 3249537024 | bytes 13156352 | tf_op jit(solution)/shard_map/dot_general | solution.py:64
  20.1 2.3 fusion.56
  22.4 1.2 copy-done.3
  23.6 2.6 copy.28
  26.2 2.6 copy.29
  28.8 2.8 concatenate.10
  31.6 1.3 concatenate.11
  32.8 1.6 copy.27
  34.6 74.4 %while.11 = (s32[]{:T(128)}, f32[12,512,128]{2,1,0:T(8,128)}, s32[12]{0:T(128)S(1)}, s32[6144]{0:T(1024)S(1)}, s32[6272]{0:T(1024)S(1)}, /*index=5*/bf16[6144,12...) while((s32[]{:T(128)}, f32[12,512,128]{2,1,0:T(8,128)}, ...), condition=%wide.region_10.11_spmd.clone, body=%wide.region_9.10_spmd.clone.sunk | while | flops 171377152 | bytes 741060 | solution.py:52
  34.6 0.6 dynamic_slice.53
  38.2 2.6 fusion.65
  40.8 0.6 dynamic_slice.53
  44.4 2.6 fusion.65
  47.0 0.6 dynamic_slice.53
  50.6 2.6 fusion.65
  53.2 0.6 dynamic_slice.53
  56.8 2.6 fusion.65
  59.4 0.6 dynamic_slice.53
  63.0 2.6 fusion.65
  69.2 2.6 fusion.65
  75.4 2.6 fusion.65
  81.6 2.6 fusion.65
  87.8 2.6 fusion.65
  90.4 0.6 dynamic_slice.53
  94.0 2.6 fusion.65
  100.2 2.6 fusion.65
  102.8 0.6 dynamic_slice.53
  106.4 2.6 fusion.65
  109.0 3.6 %fusion.55 = (f32[12,512]{1,0:T(8,128)S(1)}, f32[12,512]{1,0:T(8,128)S(1)}) fusion(f32[12,512,128]{2,1,0:T(8,128)} %get-tuple-element.54), kind=kLoop, calls=%fused_computation.120 | loop fusion | flops 2347008 | bytes 3194880 | tf_op jit(solution)/shard_map/reduce_sum | solution.py:69
  112.6 3.6 %copy.25 = f32[6144,128]{0,1:T(8,128)} copy(f32[6144,128]{1,0:T(8,128)} %bitcast.66) | data formatting | bytes 6291456 | tf_op jit(solution)/shard_map/reshape | solution.py:52
  116.2 13.3 %all-reduce.3 = (f32[6144]{0:T(1024)S(1)}, f32[6144]{0:T(1024)S(1)}) all-reduce(f32[6144]{0:T(1024)S(1)} %reduce_sum.119, f32[6144]{0:T(1024)S(1)} %reduce_sum.117), channel_id=1, replica_groups=mesh['dp'=8,'mp'=4] {'mp'}, use_global_device_ids=true, to_apply=%region_14.15 | all-reduce | flops 12288 | bytes 98304 | tf_op jit(solution)/shard_map/psum | solution.py:69
  129.5 8.8 %fusion.30 = f32[6144,512]{1,0:T(8,128)} fusion(f32[6144,128]{0,1:T(8,128)} %copy.25, bf16[6144,1,4,128]{0,3,2,1:T(8,128)(2,1)} %bitcast.68, f32[6144]{0:T(1024)S(1)} %get-tuple-element.104, f32[6144]{0:T(1024)S(1)} %get-tuple-element.103, bf16[512,512]{1,0:T(8,128)(2,1)} %param.11, s32[]{:T(128)S(6)} %select_n.164), kind=kOutput, calls=%fused_computation.39 | convolution fusion | flops 809238528 | bytes 17481732 | tf_op jit(solution)/shard_map/dot_general | solution.py:79
  138.3 12.2 %convert_element_type.24 = f32[6144,512]{1,0:T(8,128)} convert(bf16[6144,512]{1,0:T(8,128)(2,1)} %param.9) | non-fusion elementwise | flops 3145728 | bytes 18874368 | tf_op jit(solution)/shard_map/convert_element_type | solution.py:62
  151.2 20.7 %all-gather.2 = s32[8,1,24]{2,1,0:T(1,128)S(1)} all-gather(s32[1,1,24]{2,1,0:T(1,128)S(1)} %bitcast.82), channel_id=1, replica_groups=mesh['dp'=8,'mp'=4] {'dp'}, dimensions={0}, use_global_device_ids=true | all-gather | bytes 864 | tf_op jit(solution)/shard_map/all_gather | solution.py:118
  171.9 64.0 %reduce-scatter.2.cloned.1.call-done = f32[6144,128]{1,0:T(8,128)} async-done(((f32[6144,512]{1,0:T(8,128)}), f32[6144,128]{1,0:T(8,128)}) %reduce-scatter.2.cloned.1.call-update) | async-done | bytes 3145744 | tf_op jit(solution)/shard_map/reduce_scatter | solution.py:80
  235.9 3.2 add_convert_fusion
  239.1 1.9 gather_fusion
  241.0 2.8 broadcast_select_fusion
  243.8 5.7 %all-to-all-start = ((bf16[8,6,128,128]{3,2,1,0:T(8,128)(2,1)}), bf16[8,6,128,128]{3,2,1,0:T(8,128)(2,1)}, u32[]{:S(2)}, u32[]{:S(2)}) async-start(bf16[8,6,128,128]{3,2,1,0:T(8,128)(2,1)} %broadcast_select_fusion), calls=%async_computation.1 | async-start | bytes 3145728 | tf_op jit(solution)/shard_map/all_to_all | solution.py:155
  250.0 0.7 broadcast_add_fusion
  250.7 39.2 %all-gather = s32[8,1,24]{2,1,0:T(1,128)S(1)} all-gather(s32[1,1,24]{2,1,0:T(1,128)S(1)} %bitcast.80), channel_id=1, replica_groups=mesh['dp'=8,'mp'=4] {'dp'}, dimensions={0}, use_global_device_ids=true | all-gather | bytes 864 | tf_op jit(solution)/shard_map/all_gather | solution.py:119
  290.5 23.1 %all-gather.1 = s32[8,1,24]{2,1,0:T(1,128)S(1)} all-gather(s32[1,1,24]{2,1,0:T(1,128)S(1)} %bitcast.85), channel_id=1, replica_groups=mesh['dp'=8,'mp'=4] {'dp'}, dimensions={0}, use_global_device_ids=true | all-gather | bytes 864 | tf_op jit(solution)/shard_map/all_gather | solution.py:120
  313.6 0.7 reduce.8
  314.7 0.6 gather_fusion.2
  315.2 0.7 broadcast_select_fusion.1
  315.9 2.3 gather_fusion.1
  318.2 5.2 %fusion.32 = bf16[6144,128]{1,0:T(8,128)(2,1)} fusion(bf16[48,128,128]{2,1,0:T(8,128)(2,1)S(1)} %gather_fusion.1, pred[6144]{0:T(1024)(128)(4,1)S(1)} %get-tuple-element.114, pred[6144]{0:T(1024)(128)(4,1)S(1)} %get-tuple-element.113), kind=kLoop, calls=%fused_computation.42 | loop fusion | flops 1572864 | bytes 3158016 | tf_op jit(solution)/shard_map/jit(_where)/select_n | solution.py:159
  (102 shorter events, 7.3 us)
Async XLA Ops:
  7.2 4.9 %copy-start = (bf16[512,512]{1,0:T(8,128)(2,1)S(1)}, bf16[512,512]{1,0:T(8,128)(2,1)}, u32[]{:S(2)}) copy-start(bf16[512,512]{1,0:T(8,128)(2,1)} %param.10) | copy-start | bytes 1572868
  7.2 228.7 %reduce-scatter.2.cloned.1.call-start = ((), (), s32[]{:S(2)}) async-start(), calls=%async_computation.2 | async-start | bytes 15728640 | tf_op jit(solution)/shard_map/reduce_scatter | solution.py:80
  7.2 4.8 %copy-start.2 = (bf16[6144,512]{1,0:T(8,128)(2,1)S(1)}, bf16[6144,512]{1,0:T(8,128)(2,1)}, u32[]{:S(2)}) copy-start(bf16[6144,512]{1,0:T(8,128)(2,1)} %param.9) | copy-start | bytes 18874372
  20.1 3.5 %copy-start.3 = (bf16[6144,512]{0,1:T(8,128)(2,1)}, bf16[6144,512]{0,1:T(8,128)(2,1)S(1)}, u32[]{:S(2)}) copy-start(bf16[6144,512]{0,1:T(8,128)(2,1)S(1)} %multiply_convert_fusion) | copy-start | bytes 18874372
  28.8 2.8 copy-start.4
  32.8 1.6 copy-start.6
  32.8 1.6 copy-start.7
  138.3 12.2 %copy-start.5 = (s32[1,24]{1,0:T(1,128)S(1)}, s32[1,24]{1,0:T(1,128)}, u32[]{:S(2)}) copy-start(s32[1,24]{1,0:T(1,128)} %param.13) | copy-start | bytes 292
  243.8 46.7 %copy-start.8 = (s32[1,24]{1,0:T(1,128)S(1)}, s32[1,24]{1,0:T(1,128)}, u32[]{:S(2)}) copy-start(s32[1,24]{1,0:T(1,128)} %param.14) | copy-start | bytes 292
  243.8 72.1 %all-to-all-start = ((bf16[8,6,128,128]{3,2,1,0:T(8,128)(2,1)}), bf16[8,6,128,128]{3,2,1,0:T(8,128)(2,1)}, u32[]{:S(2)}, u32[]{:S(2)}) async-start(bf16[8,6,128,128]{3,2,1,0:T(8,128)(2,1)} %broadcast_select_fusion), calls=%async_computation.1 | async-start | bytes 3145728 | tf_op jit(solution)/shard_map/all_to_all | solution.py:155
  315.9 7.6 %copy-start.1 = (bf16[512,512]{1,0:T(8,128)(2,1)S(1)}, bf16[512,512]{1,0:T(8,128)(2,1)}, u32[]{:S(2)}) copy-start(bf16[512,512]{1,0:T(8,128)(2,1)} %param.10) | copy-start | bytes 1572868
Sparse Core Ops, SparseCore 0:
  138.4 97.4 reduce-scatter.1
where the time goes:
time: 331 us; the launch traced here: 330 us
  blocking collectives  96.2 us (29%)
  waiting for transfers between devices  64.1 us (19%)
  matrix products  48.1 us (15%)
  other arithmetic  34.9 us (11%)
  loops' own time  34.2 us (10%)
  local copies, waits for them, and re-layouts  32.8 us (10%)
  between operations  14.3 us (4%)
  starting transfers between devices  5.7 us (2%)
    reduce_scatter x1, waiting for transfers between devices, layer_rows(): lax.psum_scatter(partial_term, 'mp', scatter_dimension=1, tiled=True)  64 us
    all_gather x1, blocking collectives, per_device(): lax.all_gather(owner, 'dp', axis=0, tiled=True)  39.2 us
    another operation x1, loops' own time, attend(): return lax.map(one_tile, tile_starts).reshape(row_count, head_size)  34.2 us
    dot_general x12, matrix products, one_tile(): return jnp.dot(weights, value_tile, preferred_element_type=jnp.float32)  31.4 us
    all_gather x1, blocking collectives, per_device(): lax.all_gather(recv_offset, 'dp', axis=0, tiled=True)  23.1 us
    all_gather x1, blocking collectives, per_device(): lax.all_gather(hist_len, 'dp', axis=0, tiled=True)  20.7 us
    psum x1, blocking collectives, layer_rows(): lax.psum((jnp.sum(outputs, 1), jnp.sum(outputs * outputs, 1)), 'mp')  13.3 us
    convert_element_type x1, other arithmetic, layer_rows(): widened = rows_in.astype(jnp.float32)  12.2 us
  transfers between devices with their start and end apart: 2, of which 1 were waited for; matrix products, arithmetic and copies ran while one was open for 5% of the time, Pallas kernels for 0%

commit v1 on v0

v1 whole, which is shorter than its diff:
```python
import functools

import jax
import jax.numpy as jnp
from jax import lax
from jax.experimental import pallas as pl
from jax.experimental.pallas import tpu as pltpu
from jax.sharding import PartitionSpec as P

D = 512
HEADS = 4
HEAD = D // HEADS
BLOCK = 128
MAXB = 2
WIN = MAXB * BLOCK
EPS = 1e-05
MESH = pl.DeviceIdType.MESH


def norm_rows(values):
    average = jnp.mean(values, axis=-1, keepdims=True)
    variance = jnp.mean(values * values, axis=-1, keepdims=True) - average * average
    return (values - average) * lax.rsqrt(variance + EPS)


def layer_kernel(
    dp_size, mp_size, per_pair,
    table, tok_hbm, w_ref, wout_ref, meta_ref,
    arr, meta_in, state_in,
    tok, wg, wop, normed, att, gate, send, state_out,
    tok_sem, own_sem, w_send, w_recv, meta_send, meta_recv, send_sem, recv_sem,
    state_send, state_recv,
):
    d = lax.axis_index("dp")
    m = lax.axis_index("mp")
    blocks = tok_hbm.shape[0]
    quarter = D // mp_size
    reach = dp_size // mp_size
    slots = reach * per_pair

    tok_copy = pltpu.make_async_copy(tok_hbm, tok.at[pl.ds(0, blocks)], tok_sem)
    tok_copy.start()
    own_copy = pltpu.make_async_copy(w_ref, wg.at[0], own_sem)
    own_copy.start()

    barrier = pltpu.get_barrier_semaphore()

    def greet(step, carry):
        o = lax.rem(d + step // mp_size, dp_size)
        q = lax.rem(m + lax.rem(step, mp_size), mp_size)
        pl.semaphore_signal(barrier, inc=1, device_id={"dp": o, "mp": q}, device_id_type=MESH)
        return carry

    lax.fori_loop(1, dp_size * mp_size, greet, 0)
    pl.semaphore_wait(barrier, dp_size * mp_size - 1)

    def flip(bits):
        if bits == 1:
            return m + 1 - 2 * lax.rem(m, 2)
        return lax.rem(m + 2, 4)

    def w_copy(src, slot, peer, index):
        return pltpu.make_async_remote_copy(
            src_ref=src, dst_ref=wg.at[slot], send_sem=w_send.at[index],
            recv_sem=w_recv.at[index], device_id={"mp": peer}, device_id_type=MESH,
        )

    far = w_copy(w_ref, 2, flip(2), 1)
    far.start()
    near = w_copy(w_ref, 1, flip(1), 0)
    near.start()
    relay = w_copy(wg.at[2], 3, flip(1), 2)

    def meta_copy(step):
        o = lax.rem(d + step, dp_size)
        return pltpu.make_async_remote_copy(
            src_ref=meta_ref.at[o], dst_ref=meta_in.at[d], send_sem=meta_send.at[step],
            recv_sem=meta_recv.at[d], device_id={"dp": o}, device_id_type=MESH,
        )

    def start_meta(step, carry):
        meta_copy(step).start()
        return carry

    lax.fori_loop(1, dp_size, start_meta, 0)
    meta_local = pltpu.make_async_copy(meta_ref.at[d], meta_in.at[d], meta_recv.at[d])
    meta_local.start()

    tok[blocks] = jnp.zeros((BLOCK, D), jnp.bfloat16)
    for bits in range(mp_size):
        head = m
        if bits & 1:
            head = head + 1 - 2 * lax.rem(head, 2)
        if bits & 2:
            head = lax.rem(head + 2, 4)
        wop[bits * HEAD : (bits + 1) * HEAD, :] = wout_ref[
            pl.ds(pl.multiple_of(head * HEAD, HEAD), HEAD), :
        ]
    tok_copy.wait()

    def target(s):
        k = s // per_pair
        j = s - k * per_pair
        return lax.rem(d + m + mp_size * (reach - 1 - k), dp_size), j

    def rows_of(s):
        o, j = target(s)
        start = table[o, 4 * j]
        return jnp.concatenate([tok[start], tok[start + 1]], 0)

    causal = lax.broadcasted_iota(jnp.int32, (BLOCK, BLOCK), 1) <= lax.broadcasted_iota(
        jnp.int32, (BLOCK, BLOCK), 0
    )
    half_scale = 0.5 * HEAD ** (-0.5)

    def scores(q, k):
        t = lax.dot_general(
            q, k, (((1,), (1,)), ((), ())), preferred_element_type=jnp.float32
        ) * half_scale
        return t + t * jnp.tanh(t)

    def one_head(rows_in, bits):
        h = jnp.dot(rows_in, wg[bits], preferred_element_type=jnp.float32) * 0.5
        p = (h + h * jnp.tanh(h)).astype(jnp.bfloat16)
        u, v, q, k = (p[:, i * HEAD : (i + 1) * HEAD] for i in range(4))
        low = jnp.where(causal, scores(q[:BLOCK], k[:BLOCK]), 0.0).astype(jnp.bfloat16)
        back = scores(q[BLOCK:], k[:BLOCK])
        diag = jnp.where(causal, scores(q[BLOCK:], k[BLOCK:]), 0.0)
        high = jnp.concatenate([back, diag], 1).astype(jnp.bfloat16)
        first = jnp.dot(low, v[:BLOCK], preferred_element_type=jnp.float32)
        second = jnp.dot(high, v, preferred_element_type=jnp.float32)
        return u, jnp.concatenate([first, second], 0) * (1.0 / WIN)

    own_copy.wait()
    near.wait()

    def early(s, carry):
        n = norm_rows(rows_of(s).astype(jnp.float32)).astype(jnp.bfloat16)
        normed[s] = n
        for bits in (0, 1):
            u, a = one_head(n, bits)
            gate[s, bits] = u
            att[s, bits] = a
        return carry

    lax.fori_loop(0, slots, early, 0)

    far.wait()
    relay.start()
    relay.wait()

    def send_copy(s, q):
        o, j = target(s)
        return pltpu.make_async_remote_copy(
            src_ref=send.at[s, q], dst_ref=arr.at[d * per_pair + j],
            send_sem=send_sem.at[s, q], recv_sem=recv_sem.at[d * per_pair + j],
            device_id={"dp": o, "mp": q}, device_id_type=MESH,
        )

    def each_target(s, remote):
        o, j = target(s)
        for q in range(mp_size):
            own = jnp.logical_and(o == d, m == q)

            @pl.when(jnp.logical_not(own))
            def _():
                remote(s, q)

            if remote is start_send:

                @pl.when(own)
                def _():
                    pltpu.make_async_copy(
                        send.at[s, q], arr.at[d * per_pair + j], recv_sem.at[d * per_pair + j]
                    ).start()

    def start_send(s, q):
        send_copy(s, q).start()

    def end_send(s, q):
        send_copy(s, q).wait_send()

    picks = lax.broadcasted_iota(jnp.int32, (8, WIN), 1)

    def late(s, carry):
        n = normed[s]
        parts = [(gate[s, 0], att[s, 0]), (gate[s, 1], att[s, 1])]
        parts += [one_head(n, 2), one_head(n, 3)]
        a = jnp.concatenate([part[1] for part in parts], 1)
        g = jnp.concatenate([part[0] for part in parts], 1).astype(jnp.float32)
        gated = (norm_rows(a) * g).astype(jnp.bfloat16)
        y = jnp.dot(gated, wop[...], preferred_element_type=jnp.float32)
        y = (y + rows_of(s).astype(jnp.float32)).astype(jnp.bfloat16)
        o, j = target(s)
        last = table[o, 4 * j + 1] - 1
        pick = (picks == last).astype(jnp.bfloat16)
        chosen = jnp.dot(pick, y, preferred_element_type=jnp.float32)
        for q in range(mp_size):
            send[s, q] = y[:, q * quarter : (q + 1) * quarter]
            state_out[q, pl.ds(s, 1), :] = chosen[0:1, q * quarter : (q + 1) * quarter]
        each_target(s, start_send)
        return carry

    lax.fori_loop(0, slots, late, 0)

    def state_copy(step):
        q = lax.rem(m + step, mp_size)
        return pltpu.make_async_remote_copy(
            src_ref=state_out.at[q], dst_ref=state_in.at[m], send_sem=state_send.at[step],
            recv_sem=state_recv.at[m], device_id={"mp": q}, device_id_type=MESH,
        )

    for step in range(1, mp_size):
        state_copy(step).start()
    state_local = pltpu.make_async_copy(state_out.at[m], state_in.at[m], state_recv.at[m])
    state_local.start()

    def end_meta(step, carry):
        meta_copy(step).wait_send()
        return carry

    lax.fori_loop(1, dp_size, end_meta, 0)

    def got_meta(src, carry):
        pltpu.make_async_copy(meta_ref.at[src], meta_in.at[src], meta_recv.at[src]).wait()
        return carry

    lax.fori_loop(0, dp_size, got_meta, 0)

    def sent(s, carry):
        each_target(s, end_send)
        return carry

    lax.fori_loop(0, slots, sent, 0)

    def got(i, carry):
        pltpu.make_async_copy(send.at[0, 0], arr.at[i], recv_sem.at[i]).wait()
        return carry

    lax.fori_loop(0, dp_size * per_pair, got, 0)
    for step in range(1, mp_size):
        state_copy(step).wait_send()
    for q in range(mp_size):
        pltpu.make_async_copy(state_out.at[q], state_in.at[q], state_recv.at[q]).wait()


def place_kernel(dp_size, per_pair, meta, user_pos, arr, state_in, packed, state, rows32):
    slots = state_in.shape[1]
    packed[...] = jnp.zeros(packed.shape, packed.dtype)
    row = lax.broadcasted_iota(jnp.int32, (BLOCK, packed.shape[1]), 0)

    def one(i, carry):
        src = i // per_pair
        j = i - src * per_pair
        length = meta[src, 0, 4 * j + 1]
        offset = meta[src, 0, 4 * j + 2]
        for b in range(MAXB):
            fill = length - b * BLOCK

            @pl.when(fill > 0)
            def _():
                value = arr[i, b * BLOCK : (b + 1) * BLOCK, :].astype(jnp.float32)
                value = jnp.where(row < fill, value, 0.0).astype(packed.dtype)
                packed[pl.ds(pl.multiple_of((offset + b) * BLOCK, BLOCK), BLOCK), :] = value

        return carry

    lax.fori_loop(0, dp_size * per_pair, one, 0)

    def pick(u, carry):
        pos = user_pos[u]
        q = pos // slots
        rows32[pl.ds(u, 1), :] = state_in[q, pl.ds(pos - q * slots, 1), :]
        return carry

    lax.fori_loop(0, state.shape[0], pick, 0)
    state[...] = rows32[...].astype(state.dtype)


def per_device(tokens, w_uvqk, w_out, hist_len, owner, recv_offset, block_start):
    dp_size = lax.axis_size("dp")
    mp_size = lax.axis_size("mp")
    d = lax.axis_index("dp")
    user_count = hist_len.shape[1]
    per_pair = -(-user_count // dp_size)
    pairs = dp_size * per_pair
    slots = (dp_size // mp_size) * per_pair
    slots_pad = -(-slots // 8) * 8
    quarter = D // mp_size
    rows = tokens.shape[0]
    lengths, owners, offsets, starts = hist_len[0], owner[0], recv_offset[0], block_start[0]
    ids = jnp.arange(user_count, dtype=jnp.int32)
    earlier = (owners[:, None] == owners[None, :]) & (ids[None, :] < ids[:, None])
    rank = jnp.sum(earlier.astype(jnp.int32), axis=1)
    lane = jnp.arange(128, dtype=jnp.int32)
    dest = jnp.arange(dp_size, dtype=jnp.int32)
    field = lane % 4
    value = jnp.where(
        field[None, :] == 0,
        starts[:, None],
        jnp.where(field[None, :] == 1, lengths[:, None], offsets[:, None]),
    )
    match = (owners[:, None, None] == dest[None, :, None]) & (
        rank[:, None, None] == (lane // 4)[None, None, :]
    )
    meta = jnp.sum(jnp.where(match, value[:, None, :], 0), axis=0)
    relative = lax.rem(owners - d + dp_size, dp_size)
    turn = dp_size // mp_size - 1 - relative // mp_size
    user_pos = lax.rem(relative, mp_size) * slots_pad + turn * per_pair + rank

    vmem = pl.BlockSpec(memory_space=pltpu.VMEM)
    smem = pl.BlockSpec(memory_space=pltpu.SMEM)
    anywhere = pl.BlockSpec(memory_space=pl.ANY)
    bf16, f32 = jnp.bfloat16, jnp.float32
    dma = pltpu.SemaphoreType.DMA
    arr, meta_in, state_in = pl.pallas_call(
        functools.partial(layer_kernel, dp_size, mp_size, per_pair),
        out_shape=(
            jax.ShapeDtypeStruct((pairs, WIN, quarter), bf16),
            jax.ShapeDtypeStruct((dp_size, 1, 128), jnp.int32),
            jax.ShapeDtypeStruct((mp_size, slots_pad, quarter), f32),
        ),
        in_specs=[smem, anywhere, vmem, vmem, vmem],
        out_specs=(anywhere, anywhere, anywhere),
        scratch_shapes=[
            pltpu.VMEM((rows // BLOCK + 1, BLOCK, D), bf16),
            pltpu.VMEM((mp_size, D, 4 * HEAD), bf16),
            pltpu.VMEM((D, D), bf16),
            pltpu.VMEM((slots, WIN, D), bf16),
            pltpu.VMEM((slots, 2, WIN, HEAD), f32),
            pltpu.VMEM((slots, 2, WIN, HEAD), bf16),
            pltpu.VMEM((slots, mp_size, WIN, quarter), bf16),
            pltpu.VMEM((mp_size, slots_pad, quarter), f32),
            dma,
            dma,
            dma((3,)),
            dma((3,)),
            dma((dp_size,)),
            dma((dp_size,)),
            dma((slots, mp_size)),
            dma((pairs,)),
            dma((mp_size,)),
            dma((mp_size,)),
        ],
        compiler_params=pltpu.CompilerParams(
            collective_id=0, has_side_effects=True, vmem_limit_bytes=60 * 1024 * 1024
        ),
        name="layer",
    )(meta, tokens.reshape(rows // BLOCK, BLOCK, D), w_uvqk, w_out, meta.reshape(dp_size, 1, 128))
    return pl.pallas_call(
        functools.partial(place_kernel, dp_size, per_pair),
        out_shape=(
            jax.ShapeDtypeStruct((rows, quarter), bf16),
            jax.ShapeDtypeStruct((user_count, quarter), bf16),
        ),
        in_specs=[smem, smem, vmem, vmem],
        out_specs=(vmem, vmem),
        scratch_shapes=[pltpu.VMEM((user_count, quarter), f32)],
        name="place",
    )(meta_in, user_pos, arr, state_in)


def solution(mesh):
    in_specs = (
        P("dp", None),
        P(None, "mp"),
        P(),
        P("dp", None),
        P("dp", None),
        P("dp", None),
        P("dp", None),
    )
    out_specs = (P("dp", "mp"), P("dp", "mp"))
    return jax.shard_map(
        per_device, mesh=mesh, in_specs=in_specs, out_specs=out_specs, check_vma=False
    )
```

time: 331 us -> 69.5 us (0.21)
  blocking collectives: 96.2 us -> 0 us
  Pallas kernels: 0 us -> 64.2 us
  waiting for transfers between devices: 64.1 us -> 0 us
  matrix products: 48.1 us -> 0 us
  loops' own time: 34.2 us -> 0 us
  local copies, waits for them, and re-layouts: 32.8 us -> 0 us
  other arithmetic: 34.9 us -> 4.39 us
  between operations: 14.3 us -> 0.65 us
  starting transfers between devices: 5.7 us -> 0 us
    all_gather x3 -> x0, blocking collectives: 83 us -> none  [the longest x1 39.2 us: per_device(): lax.all_gather(owner, 'dp', axis=0, tiled=True)]
    pallas_call x0 -> x2, Pallas kernels: none -> 64.2 us  [the longest x1 60.1 us: per_device(): pl.pallas_call(functools.partial(layer_kernel, dp_size, mp_size, per_pair...]
    reduce_scatter x1 -> x0, waiting for transfers between devices: 64 us -> none  [layer_rows(): lax.psum_scatter(partial_term, 'mp', scatter_dimension=1, tiled=True)]
    dot_general x14 -> x0, matrix products: 48.1 us -> none  [the longest x12 31.4 us: one_tile(): return jnp.dot(weights, value_tile, preferred_element_type=jnp.float32)]
    another operation x1 -> x0, loops' own time: 34.2 us -> none  [attend(): return lax.map(one_tile, tile_starts).reshape(row_count, head_size)]
    convert_element_type x2 -> x0, other arithmetic: 15.3 us -> none  [the longest x1 12.2 us: layer_rows(): widened = rows_in.astype(jnp.float32)]
    psum x1 -> x0, blocking collectives: 13.3 us -> none  [layer_rows(): lax.psum((jnp.sum(outputs, 1), jnp.sum(outputs * outputs, 1)), 'mp')]
    dynamic_slice x36 -> x0, local copies, waits for them, and re-layouts: 8.78 us -> none  [the longest x12 6.89 us: attend(): return lax.map(one_tile, tile_starts).reshape(row_count, head_size)]
  transfers between devices with their start and end apart: 2 -> 0, of which waited for: 1 -> 0; matrix products, arithmetic and copies ran while one was open for 5% -> 0% of each run, Pallas kernels for 0% -> 0%
where the time goes in v1:
time: 69.5 us; the launch traced here: 69.3 us
  Pallas kernels  64.2 us (92%)
  other arithmetic  4.39 us (6%)
    pallas_call x1, Pallas kernels, per_device(): pl.pallas_call(functools.partial(layer_kernel, dp_size, mp_size, per_pair...  60.1 us
    pallas_call x1, Pallas kernels, per_device(): pl.pallas_call(functools.partial(place_kernel, dp_size, per_pair), out_sh...  4.13 us

profile of v1, /device:TPU:0, one launch (start us, length us, event | category | flops | bytes accessed | tf_op | source)
XLA Modules:
  0.0 69.3 jit_solution(353232177386084864)
XLA Ops:
  0.6 0.9 %convert_reduce_fusion = s32[24]{0:T(128)S(1)} fusion(s32[24]{0:T(128)} %bitcast.9), kind=kLoop, calls=%fused_computation.2 | loop fusion | flops 2856 | bytes 192 | tf_op jit(solution)/shard_map/reduce_sum | solution.py:294
  1.5 1.2 %add_add_fusion.user_pos = s32[24]{0:T(128)} fusion(s32[24]{0:T(128)S(1)} %convert_reduce_fusion, s32[]{:T(128)S(6)} %axis_index.15, s32[1,24]{1,0:T(1,128)} %param.11), kind=kLoop, calls=%fused_computation.19 | loop fusion | flops 672 | bytes 292 | tf_op jit(solution)/shard_map/add | solution.py:309
  2.8 0.1 broadcast_compare_fusion
  2.8 0.7 %iota_compare_fusion.1 = pred[24,8]{1,0:T(8,128)(4,1)S(1)} fusion(s32[24]{0:T(128)} %bitcast.10), kind=kLoop, calls=%fused_computation.4 | loop fusion | flops 192 | bytes 288 | tf_op jit(solution)/shard_map/eq | solution.py:303
  3.6 0.8 %select_select_fusion = s32[24,128]{1,0:T(8,128)S(1)} fusion(s32[24]{0:T(128)} %bitcast.11, s32[24]{0:T(128)} %bitcast.12, s32[24]{0:T(128)} %bitcast.13, pred[128]{0:T(512)(128)(4,1)S(1)} %get-tuple-element.9, pred[128]{0:T(512)(128)(4,1)S(1)} %get-tuple-element.8), kind=kLoop, calls=%fused_computation.1 | loop fusion | flops 6144 | bytes 12832 | tf_op jit(solution)/shard_map/jit(_where)/select_n | solution.py:298
  4.3 0.7 %select_reduce_fusion.table = s32[8,128]{1,0:T(8,128)} fusion(s32[24,128]{1,0:T(8,128)S(1)} %select_select_fusion, pred[24,128]{1,0:T(8,128)(4,1)S(1)} %broadcast_compare_fusion, pred[24,8]{1,0:T(8,128)(4,1)S(1)} %iota_compare_fusion.1), kind=kLoop, calls=%fused_computation | loop fusion | flops 72704 | bytes 19648 | tf_op jit(solution)/shard_map/reduce_sum | solution.py:306
  5.0 60.1 %layer.1 = (bf16[24,256,128]{2,1,0:T(8,128)(2,1)}, s32[8,1,128]{2,1,0:T(1,128)}, f32[4,8,128]{2,1,0:T(8,128)}) custom-call(s32[8,128]{1,0:T(8,128)} %select_reduce_fusion.table, bf16[48,128,512]{2,1,0:T(8,128)(2,1)} %bitcast.7, bf16[512,512]{1,0:T(8,128)(2,1)} %w_ref.1, bf16[512,512]{1,0:T(8,128)(2,1)} %wout_ref.1, s32[8,1,128]{2,1,0:T(1,128)} %bitcast.8), custom_call_target="tpu_custom_call" | custom-call | tf_op jit(solution)/shard_map/layer/pallas_call | solution.py:316
  65.1 4.1 %place.1 = (bf16[6144,128]{1,0:T(8,128)(2,1)}, bf16[24,128]{1,0:T(8,128)(2,1)}) custom-call(s32[8,1,128]{2,1,0:T(1,128)} %get-tuple-element.5.meta, s32[24]{0:T(128)} %add_add_fusion.user_pos, bf16[24,256,128]{2,1,0:T(8,128)(2,1)} %get-tuple-element.6.arr, f32[4,8,128]{2,1,0:T(8,128)} %get-tuple-element.7.state_in), custom_call_target="tpu_custom_call" | custom-call | tf_op jit(solution)/shard_map/place/pallas_call | solution.py:350
  (2 shorter events, 0.0 us)

commit v2 on v1

v2 whole, which is shorter than its diff:
```python
import functools

import jax
import jax.numpy as jnp
from jax import lax
from jax.experimental import pallas as pl
from jax.experimental.pallas import tpu as pltpu
from jax.sharding import PartitionSpec as P

D = 512
HEADS = 4
HEAD = D // HEADS
BLOCK = 128
MAXB = 2
WIN = MAXB * BLOCK
EPS = 1e-05
MESH = pl.DeviceIdType.MESH


def norm_rows(values):
    average = jnp.mean(values, axis=-1, keepdims=True)
    variance = jnp.mean(values * values, axis=-1, keepdims=True) - average * average
    return (values - average) * lax.rsqrt(variance + EPS)


def gather_kernel(
    dp_size, mp_size, per_pair,
    owner, hist_len, recv_offset, block_start, tok_hbm,
    table, user_pos, picked, row_sem,
):
    d = lax.axis_index("dp")
    m = lax.axis_index("mp")
    last_block = tok_hbm.shape[0] - 1
    slots = picked.shape[0]
    slots_pad = -(-per_pair // 8) * 8

    def clear(o, carry):
        for lane in range(4 * per_pair):
            table[o, 0, lane] = 0
        return carry

    lax.fori_loop(0, dp_size, clear, 0)

    def enter(u, carry):
        o = owner[0, u]
        rank = table[o, 0, 3]
        table[o, 0, 3] = rank + 1
        table[o, 0, 4 * rank] = block_start[0, u]
        table[o, 0, 4 * rank + 1] = hist_len[0, u]
        table[o, 0, 4 * rank + 2] = recv_offset[0, u]
        user_pos[u] = o * slots_pad + rank
        return carry

    lax.fori_loop(0, user_pos.shape[0], enter, 0)

    def copy(s, b):
        k = s // per_pair
        o = lax.rem(d + m + mp_size * k, dp_size)
        start = table[o, 0, 4 * (s - k * per_pair)]
        return pltpu.make_async_copy(
            tok_hbm.at[jnp.minimum(start + b, last_block)], picked.at[s, b], row_sem.at[s, b]
        )

    def begin(s, carry):
        for b in range(MAXB):
            copy(s, b).start()
        return carry

    def end(s, carry):
        for b in range(MAXB):
            copy(s, b).wait()
        return carry

    lax.fori_loop(0, slots, begin, 0)
    lax.fori_loop(0, slots, end, 0)


def layer_kernel(
    dp_size, mp_size, per_pair,
    rows_ref, w_ref, wout_ref, meta_ref,
    arr, meta_out, state_in,
    xin, wg, wop, send, state_out, meta_in,
    own_sem, w_send, w_recv, meta_send, meta_recv, row_send, row_recv, send_sem, recv_sem,
    state_send, state_recv, out_sem,
):
    d = lax.axis_index("dp")
    m = lax.axis_index("mp")
    quarter = D // mp_size
    reach = dp_size // mp_size
    slots = reach * per_pair

    own_copy = pltpu.make_async_copy(w_ref, wg.at[0], own_sem)
    own_copy.start()

    barrier = pltpu.get_barrier_semaphore()

    def greet(step, carry):
        o = lax.rem(d + step // mp_size, dp_size)
        q = lax.rem(m + lax.rem(step, mp_size), mp_size)
        pl.semaphore_signal(barrier, inc=1, device_id={"dp": o, "mp": q}, device_id_type=MESH)
        return carry

    lax.fori_loop(1, dp_size * mp_size, greet, 0)
    pl.semaphore_wait(barrier, dp_size * mp_size - 1)

    def flip(bits):
        if bits == 1:
            return m + 1 - 2 * lax.rem(m, 2)
        return lax.rem(m + 2, 4)

    def w_copy(src, slot, peer, index):
        return pltpu.make_async_remote_copy(
            src_ref=src, dst_ref=wg.at[slot], send_sem=w_send.at[index],
            recv_sem=w_recv.at[index], device_id={"mp": peer}, device_id_type=MESH,
        )

    far = w_copy(w_ref, 2, flip(2), 1)
    far.start()
    near = w_copy(w_ref, 1, flip(1), 0)
    near.start()
    relay = w_copy(wg.at[2], 3, flip(1), 2)

    def target(s):
        k = s // per_pair
        return lax.rem(d + m + mp_size * k, dp_size)

    def source(s):
        k = s // per_pair
        return lax.rem(d - m - mp_size * k + 2 * dp_size, dp_size), s - k * per_pair

    def row_copy(s):
        return pltpu.make_async_remote_copy(
            src_ref=rows_ref.at[s], dst_ref=xin.at[s], send_sem=row_send.at[s],
            recv_sem=row_recv.at[s], device_id={"dp": target(s)}, device_id_type=MESH,
        )

    def row_local(s):
        return pltpu.make_async_copy(rows_ref.at[s], xin.at[s], row_recv.at[s])

    def start_rows(s, carry):
        here = target(s) == d

        @pl.when(jnp.logical_not(here))
        def _():
            row_copy(s).start()

        @pl.when(here)
        def _():
            row_local(s).start()

        return carry

    def end_rows(s, carry):
        @pl.when(target(s) != d)
        def _():
            row_copy(s).wait_send()

        return carry

    lax.fori_loop(0, slots, start_rows, 0)

    def meta_copy(step):
        o = lax.rem(d + step, dp_size)
        return pltpu.make_async_remote_copy(
            src_ref=meta_ref.at[o], dst_ref=meta_in.at[d], send_sem=meta_send.at[step],
            recv_sem=meta_recv.at[d], device_id={"dp": o}, device_id_type=MESH,
        )

    def start_meta(step, carry):
        meta_copy(step).start()
        return carry

    lax.fori_loop(1, dp_size, start_meta, 0)
    pltpu.make_async_copy(meta_ref.at[d], meta_in.at[d], meta_recv.at[d]).start()

    for bits in range(mp_size):
        head = m
        if bits & 1:
            head = head + 1 - 2 * lax.rem(head, 2)
        if bits & 2:
            head = lax.rem(head + 2, 4)
        wop[bits * HEAD : (bits + 1) * HEAD, :] = wout_ref[
            pl.ds(pl.multiple_of(head * HEAD, HEAD), HEAD), :
        ]

    causal = lax.broadcasted_iota(jnp.int32, (BLOCK, BLOCK), 1) <= lax.broadcasted_iota(
        jnp.int32, (BLOCK, BLOCK), 0
    )
    half_scale = 0.5 * HEAD ** (-0.5)

    def scores(q, k):
        t = lax.dot_general(
            q, k, (((1,), (1,)), ((), ())), preferred_element_type=jnp.float32
        ) * half_scale
        return t + t * jnp.tanh(t)

    def one_head(rows_in, bits):
        h = jnp.dot(rows_in, wg[bits], preferred_element_type=jnp.float32) * 0.5
        p = (h + h * jnp.tanh(h)).astype(jnp.bfloat16)
        u, v, q, k = (p[:, i * HEAD : (i + 1) * HEAD] for i in range(4))
        low = jnp.where(causal, scores(q[:BLOCK], k[:BLOCK]), 0.0).astype(jnp.bfloat16)
        back = scores(q[BLOCK:], k[:BLOCK])
        diag = jnp.where(causal, scores(q[BLOCK:], k[BLOCK:]), 0.0)
        high = jnp.concatenate([back, diag], 1).astype(jnp.bfloat16)
        first = jnp.dot(low, v[:BLOCK], preferred_element_type=jnp.float32)
        second = jnp.dot(high, v, preferred_element_type=jnp.float32)
        return u, jnp.concatenate([first, second], 0) * (1.0 / WIN)

    def got_meta(src, carry):
        pltpu.make_async_copy(meta_ref.at[src], meta_in.at[src], meta_recv.at[src]).wait()
        return carry

    lax.fori_loop(0, dp_size, got_meta, 0)
    meta_back = pltpu.make_async_copy(meta_in, meta_out, out_sem)
    meta_back.start()

    own_copy.wait()
    near.wait()
    far.wait()
    relay.start()
    relay.wait()

    def send_copy(s, q):
        src, j = source(s)
        pair = src * per_pair + j
        return pltpu.make_async_remote_copy(
            src_ref=send.at[s, q], dst_ref=arr.at[pair], send_sem=send_sem.at[s, q],
            recv_sem=recv_sem.at[pair], device_id={"mp": q}, device_id_type=MESH,
        )

    picks = lax.broadcasted_iota(jnp.int32, (8, WIN), 1)
    lanes = lax.broadcasted_iota(jnp.int32, (1, 128), 1)

    def one_user(s, carry):
        row_local(s).wait()
        src, j = source(s)
        rows_in = xin[s].reshape(WIN, D).astype(jnp.float32)
        n = norm_rows(rows_in).astype(jnp.bfloat16)
        parts = [one_head(n, bits) for bits in range(mp_size)]
        a = jnp.concatenate([part[1] for part in parts], 1)
        g = jnp.concatenate([part[0] for part in parts], 1).astype(jnp.float32)
        gated = (norm_rows(a) * g).astype(jnp.bfloat16)
        y = jnp.dot(gated, wop[...], preferred_element_type=jnp.float32)
        y = (y + rows_in).astype(jnp.bfloat16)
        length = jnp.sum(
            jnp.where(lanes == 4 * j + 1, meta_in[src], 0), axis=1, keepdims=True
        )
        pick = jnp.where(picks == length - 1, 1.0, 0.0).astype(jnp.bfloat16)
        chosen = jnp.dot(pick, y, preferred_element_type=jnp.float32)
        for q in range(mp_size):
            send[s, q] = y[:, q * quarter : (q + 1) * quarter]
            state_out[s // per_pair, q, pl.ds(j, 1), :] = chosen[
                0:1, q * quarter : (q + 1) * quarter
            ]
        pair = src * per_pair + j
        for q in range(mp_size):

            @pl.when(m != q)
            def _():
                send_copy(s, q).start()

            @pl.when(m == q)
            def _():
                pltpu.make_async_copy(send.at[s, q], arr.at[pair], recv_sem.at[pair]).start()

        return carry

    lax.fori_loop(0, slots, one_user, 0)

    def state_step(step, first):
        k = step // mp_size
        q = step - k * mp_size
        src, _ = source(k * per_pair)
        own = jnp.logical_and(src == d, q == m)

        @pl.when(jnp.logical_not(own))
        def _():
            copy = pltpu.make_async_remote_copy(
                src_ref=state_out.at[k, q], dst_ref=state_in.at[d],
                send_sem=state_send.at[step], recv_sem=state_recv.at[d],
                device_id={"dp": src, "mp": q}, device_id_type=MESH,
            )
            if first:
                copy.start()
            else:
                copy.wait_send()

        if first:

            @pl.when(own)
            def _():
                pltpu.make_async_copy(
                    state_out.at[k, q], state_in.at[d], state_recv.at[d]
                ).start()

    def start_state(step, carry):
        state_step(step, True)
        return carry

    def end_state(step, carry):
        state_step(step, False)
        return carry

    lax.fori_loop(0, reach * mp_size, start_state, 0)
    meta_back.wait()

    def end_meta(step, carry):
        meta_copy(step).wait_send()
        return carry

    lax.fori_loop(1, dp_size, end_meta, 0)
    lax.fori_loop(0, slots, end_rows, 0)

    def sent(s, carry):
        for q in range(mp_size):

            @pl.when(m != q)
            def _():
                send_copy(s, q).wait_send()

        return carry

    lax.fori_loop(0, slots, sent, 0)
    lax.fori_loop(0, reach * mp_size, end_state, 0)

    def got(i, carry):
        pltpu.make_async_copy(send.at[0, 0], arr.at[i], recv_sem.at[i]).wait()
        return carry

    lax.fori_loop(0, dp_size * per_pair, got, 0)

    def got_state(o, carry):
        pltpu.make_async_copy(state_out.at[0, 0], state_in.at[o], state_recv.at[o]).wait()
        return carry

    lax.fori_loop(0, dp_size, got_state, 0)


def place_kernel(dp_size, per_pair, meta, user_pos, arr, state_in, packed, state, rows32):
    slots = state_in.shape[1]
    packed[...] = jnp.zeros(packed.shape, packed.dtype)
    row = lax.broadcasted_iota(jnp.int32, (BLOCK, packed.shape[1]), 0)

    def one(i, carry):
        src = i // per_pair
        j = i - src * per_pair
        length = meta[src, 0, 4 * j + 1]
        offset = meta[src, 0, 4 * j + 2]
        for b in range(MAXB):
            fill = length - b * BLOCK

            @pl.when(fill > 0)
            def _():
                value = arr[i, b * BLOCK : (b + 1) * BLOCK, :].astype(jnp.float32)
                value = jnp.where(row < fill, value, 0.0).astype(packed.dtype)
                packed[pl.ds(pl.multiple_of((offset + b) * BLOCK, BLOCK), BLOCK), :] = value

        return carry

    lax.fori_loop(0, dp_size * per_pair, one, 0)

    def pick(u, carry):
        pos = user_pos[u]
        q = pos // slots
        rows32[pl.ds(u, 1), :] = state_in[q, pl.ds(pos - q * slots, 1), :]
        return carry

    lax.fori_loop(0, state.shape[0], pick, 0)
    state[...] = rows32[...].astype(state.dtype)


def per_device(tokens, w_uvqk, w_out, hist_len, owner, recv_offset, block_start):
    dp_size = lax.axis_size("dp")
    mp_size = lax.axis_size("mp")
    user_count = hist_len.shape[1]
    per_pair = -(-user_count // dp_size)
    pairs = dp_size * per_pair
    reach = dp_size // mp_size
    slots = reach * per_pair
    slots_pad = -(-per_pair // 8) * 8
    quarter = D // mp_size
    rows = tokens.shape[0]

    vmem = pl.BlockSpec(memory_space=pltpu.VMEM)
    smem = pl.BlockSpec(memory_space=pltpu.SMEM)
    anywhere = pl.BlockSpec(memory_space=pl.ANY)
    bf16, f32 = jnp.bfloat16, jnp.float32
    dma = pltpu.SemaphoreType.DMA
    meta, user_pos, picked = pl.pallas_call(
        functools.partial(gather_kernel, dp_size, mp_size, per_pair),
        out_shape=(
            jax.ShapeDtypeStruct((dp_size, 1, 128), jnp.int32),
            jax.ShapeDtypeStruct((user_count,), jnp.int32),
            jax.ShapeDtypeStruct((slots, MAXB, BLOCK, D), bf16),
        ),
        in_specs=[smem, smem, smem, smem, anywhere],
        out_specs=(smem, smem, vmem),
        scratch_shapes=[dma((slots, MAXB))],
        name="gather",
    )(owner, hist_len, recv_offset, block_start, tokens.reshape(rows // BLOCK, BLOCK, D))
    arr, meta_in, state_in = pl.pallas_call(
        functools.partial(layer_kernel, dp_size, mp_size, per_pair),
        out_shape=(
            jax.ShapeDtypeStruct((pairs, WIN, quarter), bf16),
            jax.ShapeDtypeStruct((dp_size, 1, 128), jnp.int32),
            jax.ShapeDtypeStruct((dp_size, slots_pad, quarter), f32),
        ),
        in_specs=[anywhere, vmem, vmem, vmem],
        out_specs=(anywhere, anywhere, anywhere),
        scratch_shapes=[
            pltpu.VMEM((slots, MAXB, BLOCK, D), bf16),
            pltpu.VMEM((mp_size, D, 4 * HEAD), bf16),
            pltpu.VMEM((D, D), bf16),
            pltpu.VMEM((slots, mp_size, WIN, quarter), bf16),
            pltpu.VMEM((reach, mp_size, slots_pad, quarter), f32),
            pltpu.VMEM((dp_size, 1, 128), jnp.int32),
            dma,
            dma((3,)),
            dma((3,)),
            dma((dp_size,)),
            dma((dp_size,)),
            dma((slots,)),
            dma((slots,)),
            dma((slots, mp_size)),
            dma((pairs,)),
            dma((reach * mp_size,)),
            dma((dp_size,)),
            dma,
        ],
        compiler_params=pltpu.CompilerParams(
            collective_id=0, has_side_effects=True, vmem_limit_bytes=40 * 1024 * 1024
        ),
        name="layer",
    )(picked, w_uvqk, w_out, meta)
    return pl.pallas_call(
        functools.partial(place_kernel, dp_size, per_pair),
        out_shape=(
            jax.ShapeDtypeStruct((rows, quarter), bf16),
            jax.ShapeDtypeStruct((user_count, quarter), bf16),
        ),
        in_specs=[smem, smem, vmem, vmem],
        out_specs=(vmem, vmem),
        scratch_shapes=[pltpu.VMEM((user_count, quarter), f32)],
        name="place",
    )(meta_in, user_pos, arr, state_in)


def solution(mesh):
    in_specs = (
        P("dp", None),
        P(None, "mp"),
        P(),
        P("dp", None),
        P("dp", None),
        P("dp", None),
        P("dp", None),
    )
    out_specs = (P("dp", "mp"), P("dp", "mp"))
    return jax.shard_map(
        per_device, mesh=mesh, in_specs=in_specs, out_specs=out_specs, check_vma=False
    )
```

time: 69.5 us -> 79.8 us (1.15)
  Pallas kernels: 64.2 us -> 74.2 us
  local copies, waits for them, and re-layouts: 0 us -> 4.43 us
  other arithmetic: 4.39 us -> 0 us
    pallas_call x1, Pallas kernels: 60.1 us -> 65.9 us  [per_device(): pl.pallas_call(functools.partial(layer_kernel, dp_size, mp_size, per_pair...]
    unnamed x0 -> x14, local copies, waits for them, and re-layouts: none -> 4.43 us
    pallas_call x0 -> x1, Pallas kernels: none -> 4.1 us  [per_device(): pl.pallas_call(functools.partial(gather_kernel, dp_size, mp_size, per_pai...]
    reduce_sum x2 -> x0, other arithmetic: 1.61 us -> none  [the longest x1 0.91 us: per_device(): rank = jnp.sum(earlier.astype(jnp.int32), axis=1)]
    add x1 -> x0, other arithmetic: 1.21 us -> none  [per_device(): user_pos = lax.rem(relative, mp_size) * slots_pad + turn * per_pair + rank]
    eq x3 -> x0, other arithmetic: 0.81 us -> none  [the longest x1 0.73 us: per_device(): owners[:, None, None] == dest[None, :, None]]
where the time goes in v2:
time: 79.8 us; the launch traced here: 79.3 us
  Pallas kernels  74.2 us (93%)
  local copies, waits for them, and re-layouts  4.43 us (6%)
    pallas_call x1, Pallas kernels, per_device(): pl.pallas_call(functools.partial(layer_kernel, dp_size, mp_size, per_pair...  65.9 us
    unnamed x14, local copies, waits for them, and re-layouts  4.43 us
    pallas_call x1, Pallas kernels, per_device(): pl.pallas_call(functools.partial(place_kernel, dp_size, per_pair), out_sh...  4.12 us
    pallas_call x1, Pallas kernels, per_device(): pl.pallas_call(functools.partial(gather_kernel, dp_size, mp_size, per_pai...  4.1 us

profile of v2, /device:TPU:0, one launch (start us, length us, event | category | flops | bytes accessed | tf_op | source)
XLA Modules:
  0.0 79.3 jit_solution(16708357626988942641)
XLA Ops:
  0.6 0.0 copy-start.2
  0.6 0.0 copy-start.3
  0.7 4.1 %gather.1 = (s32[8,1,128]{2,1,0:T(1,128)}, s32[24]{0:T(128)}, bf16[6,2,128,512]{3,2,1,0:T(8,128)(2,1)}) custom-call(s32[1,24]{1,0:T(1,128)} %owner.1, s32[1,24]{1,0:T(1,128)} %hist_len.1, s32[1,24]{1,0:T(1,128)} %recv_offset.1, s32[1,24]{1,0:T(1,128)} %block_start.1, bf16[48,128,512]{2,1,0:T(8,128)(2,1)} %bitcast.1), custom_call_target="tpu_custom_call" | custom-call | tf_op jit(solution)/shard_map/gather/pallas_call | solution.py:389
  4.8 0.0 copy-done.2
  4.8 0.0 copy-done.3
  4.8 0.0 copy-start.1
  4.8 1.4 %copy-done.1 = bf16[6,2,128,512]{3,2,1,0:T(8,128)(2,1)S(1)} copy-done((bf16[6,2,128,512]{3,2,1,0:T(8,128)(2,1)S(1)}, bf16[6,2,128,512]{3,2,1,0:T(8,128)(2,1)}, u32[]{:S(2)}) %copy-start.1) | copy-done | bytes 1572888
  6.2 0.0 copy-start.6
  6.2 0.7 copy-done.6
  6.9 65.9 %layer.1 = (bf16[24,256,128]{2,1,0:T(8,128)(2,1)S(1)}, s32[8,1,128]{2,1,0:T(1,128)S(1)}, f32[8,8,128]{2,1,0:T(8,128)S(1)}) custom-call(bf16[6,2,128,512]{3,2,1,0:T(8,128)(2,1)S(1)} %copy-done.1, bf16[512,512]{1,0:T(8,128)(2,1)S(1)} %copy-done.2, bf16[512,512]{1,0:T(8,128)(2,1)S(1)} %copy-done.3, s32[8,1,128]{2,1,0:T(1,128)S(1)} %copy-done.6), custom_call_target="tpu_custom_call" | custom-call | tf_op jit(solution)/shard_map/layer/pallas_call | solution.py:401
  72.8 0.0 copy-start
  72.8 1.1 %copy-done = bf16[24,256,128]{2,1,0:T(8,128)(2,1)} copy-done((bf16[24,256,128]{2,1,0:T(8,128)(2,1)}, bf16[24,256,128]{2,1,0:T(8,128)(2,1)S(1)}, u32[]{:S(2)}) %copy-start) | copy-done | bytes 1572888
  74.0 0.0 copy-start.4
  74.0 0.6 copy-done.4
  74.6 0.0 copy-start.5
  74.6 0.6 copy-done.5
  75.2 4.1 %place.1 = (bf16[6144,128]{1,0:T(8,128)(2,1)}, bf16[24,128]{1,0:T(8,128)(2,1)}) custom-call(s32[8,1,128]{2,1,0:T(1,128)} %copy-done.5, s32[24]{0:T(128)} %get-tuple-element.11.user_pos, bf16[24,256,128]{2,1,0:T(8,128)(2,1)} %copy-done, f32[8,8,128]{2,1,0:T(8,128)} %copy-done.4), custom_call_target="tpu_custom_call" | custom-call | tf_op jit(solution)/shard_map/place/pallas_call | solution.py:435
Async XLA Ops:
  0.6 4.1 %copy-start.2 = (bf16[512,512]{1,0:T(8,128)(2,1)S(1)}, bf16[512,512]{1,0:T(8,128)(2,1)}, u32[]{:S(2)}) copy-start(bf16[512,512]{1,0:T(8,128)(2,1)} %w_ref.1) | copy-start | bytes 1572868
  0.6 4.1 %copy-start.3 = (bf16[512,512]{1,0:T(8,128)(2,1)S(1)}, bf16[512,512]{1,0:T(8,128)(2,1)}, u32[]{:S(2)}) copy-start(bf16[512,512]{1,0:T(8,128)(2,1)} %wout_ref.1) | copy-start | bytes 1572868
  4.8 1.4 %copy-start.1 = (bf16[6,2,128,512]{3,2,1,0:T(8,128)(2,1)S(1)}, bf16[6,2,128,512]{3,2,1,0:T(8,128)(2,1)}, u32[]{:S(2)}) copy-start(bf16[6,2,128,512]{3,2,1,0:T(8,128)(2,1)} %get-tuple-element.8.rows_ref) | copy-start | bytes 4718596
  6.2 0.7 copy-start.6
  72.8 1.1 %copy-start = (bf16[24,256,128]{2,1,0:T(8,128)(2,1)}, bf16[24,256,128]{2,1,0:T(8,128)(2,1)S(1)}, u32[]{:S(2)}) copy-start(bf16[24,256,128]{2,1,0:T(8,128)(2,1)S(1)} %get-tuple-element.12.arr) | copy-start | bytes 4718596
  74.0 0.6 copy-start.4
  74.6 0.6 copy-start.5

commit v3 on v2

--- a/solution.py
+++ b/solution.py
@@ -32,7 +32,6 @@
     m = lax.axis_index("mp")
     last_block = tok_hbm.shape[0] - 1
     slots = picked.shape[0]
-    slots_pad = -(-per_pair // 8) * 8
 
     def clear(o, carry):
         for lane in range(4 * per_pair):
@@ -48,7 +47,7 @@
         table[o, 0, 4 * rank] = block_start[0, u]
         table[o, 0, 4 * rank + 1] = hist_len[0, u]
         table[o, 0, 4 * rank + 2] = recv_offset[0, u]
-        user_pos[u] = o * slots_pad + rank
+        user_pos[u] = o * per_pair + rank
         return carry
 
     lax.fori_loop(0, user_pos.shape[0], enter, 0)
@@ -137,21 +136,25 @@
     def row_local(s):
         return pltpu.make_async_copy(rows_ref.at[s], xin.at[s], row_recv.at[s])
 
+    def travels(s):
+        k = s // per_pair
+        return lax.rem(s - k * per_pair + k, 2) == 0
+
     def start_rows(s, carry):
-        here = target(s) == d
-
-        @pl.when(jnp.logical_not(here))
+        away = jnp.logical_and(travels(s), target(s) != d)
+
+        @pl.when(away)
         def _():
             row_copy(s).start()
 
-        @pl.when(here)
+        @pl.when(jnp.logical_not(away))
         def _():
             row_local(s).start()
 
         return carry
 
     def end_rows(s, carry):
-        @pl.when(target(s) != d)
+        @pl.when(jnp.logical_and(travels(s), target(s) != d))
         def _():
             row_copy(s).wait_send()
 
@@ -220,20 +223,37 @@
     relay.start()
     relay.wait()
 
+    def route(s):
+        src, j = source(s)
+        moved = travels(s)
+        home = jnp.where(moved, src, d)
+        there = jnp.where(moved, d, target(s))
+        return moved, home, there, j
+
     def send_copy(s, q):
-        src, j = source(s)
-        pair = src * per_pair + j
+        _, home, there, j = route(s)
+        pair = home * per_pair + j
         return pltpu.make_async_remote_copy(
             src_ref=send.at[s, q], dst_ref=arr.at[pair], send_sem=send_sem.at[s, q],
-            recv_sem=recv_sem.at[pair], device_id={"mp": q}, device_id_type=MESH,
+            recv_sem=recv_sem.at[pair], device_id={"dp": there, "mp": q}, device_id_type=MESH,
+        )
+
+    def state_copy(s, q):
+        _, home, there, j = route(s)
+        pair = there * per_pair + j
+        return pltpu.make_async_remote_copy(
+            src_ref=state_out.at[s, q], dst_ref=state_in.at[pair], send_sem=state_send.at[s, q],
+            recv_sem=state_recv.at[pair], device_id={"dp": home, "mp": q}, device_id_type=MESH,
         )
 
     picks = lax.broadcasted_iota(jnp.int32, (8, WIN), 1)
     lanes = lax.broadcasted_iota(jnp.int32, (1, 128), 1)
-
-    def one_user(s, carry):
+    positions = lax.broadcasted_iota(jnp.int32, (WIN, D), 0)
+
+    def one_user(s):
         row_local(s).wait()
-        src, j = source(s)
+        moved, home, there, j = route(s)
+        src, _ = source(s)
         rows_in = xin[s].reshape(WIN, D).astype(jnp.float32)
         n = norm_rows(rows_in).astype(jnp.bfloat16)
         parts = [one_head(n, bits) for bits in range(mp_size)]
@@ -241,67 +261,52 @@
         g = jnp.concatenate([part[0] for part in parts], 1).astype(jnp.float32)
         gated = (norm_rows(a) * g).astype(jnp.bfloat16)
         y = jnp.dot(gated, wop[...], preferred_element_type=jnp.float32)
-        y = (y + rows_in).astype(jnp.bfloat16)
-        length = jnp.sum(
-            jnp.where(lanes == 4 * j + 1, meta_in[src], 0), axis=1, keepdims=True
-        )
+        entry = jnp.where(moved, meta_in[src], meta_ref[target(s)])
+        length = jnp.sum(jnp.where(lanes == 4 * j + 1, entry, 0), axis=1, keepdims=True)
+        y = jnp.where(positions < length, y + rows_in, 0.0).astype(jnp.bfloat16)
+        for q in range(mp_size):
+            send[s, q] = y[:, q * quarter : (q + 1) * quarter]
         pick = jnp.where(picks == length - 1, 1.0, 0.0).astype(jnp.bfloat16)
         chosen = jnp.dot(pick, y, preferred_element_type=jnp.float32)
         for q in range(mp_size):
-            send[s, q] = y[:, q * quarter : (q + 1) * quarter]
-            state_out[s // per_pair, q, pl.ds(j, 1), :] = chosen[
-                0:1, q * quarter : (q + 1) * quarter
-            ]
-        pair = src * per_pair + j
+            state_out[s, q] = chosen[:, q * quarter : (q + 1) * quarter]
+        pair = home * per_pair + j
+        state_pair = there * per_pair + j
         for q in range(mp_size):
-
-            @pl.when(m != q)
+            own = jnp.logical_and(there == d, q == m)
+
+            @pl.when(jnp.logical_not(own))
             def _():
                 send_copy(s, q).start()
 
-            @pl.when(m == q)
+            @pl.when(own)
             def _():
                 pltpu.make_async_copy(send.at[s, q], arr.at[pair], recv_sem.at[pair]).start()
 
-        return carry
-
-    lax.fori_loop(0, slots, one_user, 0)
-
-    def state_step(step, first):
-        k = step // mp_size
-        q = step - k * mp_size
-        src, _ = source(k * per_pair)
-        own = jnp.logical_and(src == d, q == m)
-
-        @pl.when(jnp.logical_not(own))
+        for q in range(mp_size):
+            own = jnp.logical_and(home == d, q == m)
+
+            @pl.when(jnp.logical_not(own))
+            def _():
+                state_copy(s, q).start()
+
+            @pl.when(own)
+            def _():
+                pltpu.make_async_copy(
+                    state_out.at[s, q], state_in.at[state_pair], state_recv.at[state_pair]
+                ).start()
+
+    def turn(i, carry):
+        late = i // slots
+        s = i - late * slots
+
+        @pl.when(travels(s) == (late == 1))
         def _():
-            copy = pltpu.make_async_remote_copy(
-                src_ref=state_out.at[k, q], dst_ref=state_in.at[d],
-                send_sem=state_send.at[step], recv_sem=state_recv.at[d],
-                device_id={"dp": src, "mp": q}, device_id_type=MESH,
-            )
-            if first:
-                copy.start()
-            else:
-                copy.wait_send()
-
-        if first:
-
-            @pl.when(own)
-            def _():
-                pltpu.make_async_copy(
-                    state_out.at[k, q], state_in.at[d], state_recv.at[d]
-                ).start()
-
-    def start_state(step, carry):
-        state_step(step, True)
-        return carry
-
-    def end_state(step, carry):
-        state_step(step, False)
-        return carry
-
-    lax.fori_loop(0, reach * mp_size, start_state, 0)
+            one_user(s)
+
+        return carry
+
+    lax.fori_loop(0, 2 * slots, turn, 0)
     meta_back.wait()
 
     def end_meta(step, carry):
@@ -312,61 +317,91 @@
     lax.fori_loop(0, slots, end_rows, 0)
 
     def sent(s, carry):
+        _, home, there, _ = route(s)
         for q in range(mp_size):
 
-            @pl.when(m != q)
+            @pl.when(jnp.logical_not(jnp.logical_and(there == d, q == m)))
             def _():
                 send_copy(s, q).wait_send()
 
+            @pl.when(jnp.logical_not(jnp.logical_and(home == d, q == m)))
+            def _():
+                state_copy(s, q).wait_send()
+
         return carry
 
     lax.fori_loop(0, slots, sent, 0)
-    lax.fori_loop(0, reach * mp_size, end_state, 0)
 
     def got(i, carry):
         pltpu.make_async_copy(send.at[0, 0], arr.at[i], recv_sem.at[i]).wait()
+        pltpu.make_async_copy(state_out.at[0, 0], state_in.at[i], state_recv.at[i]).wait()
         return carry
 
     lax.fori_loop(0, dp_size * per_pair, got, 0)
 
-    def got_state(o, carry):
-        pltpu.make_async_copy(state_out.at[0, 0], state_in.at[o], state_recv.at[o]).wait()
-        return carry
-
-    lax.fori_loop(0, dp_size, got_state, 0)
-
-
-def place_kernel(dp_size, per_pair, meta, user_pos, arr, state_in, packed, state, rows32):
-    slots = state_in.shape[1]
-    packed[...] = jnp.zeros(packed.shape, packed.dtype)
-    row = lax.broadcasted_iota(jnp.int32, (BLOCK, packed.shape[1]), 0)
+
+def place_kernel(
+    dp_size, per_pair,
+    meta, user_pos, arr, state_in,
+    packed, state,
+    held, zero, rows32, used, in_sem, out_sem,
+):
+    pairs = dp_size * per_pair
+    blocks = packed.shape[0]
+
+    def bring(i):
+        return pltpu.make_async_copy(arr.at[i], held.at[i], in_sem.at[i])
+
+    def put(source, block):
+        return pltpu.make_async_copy(source, packed.at[block], out_sem.at[block])
+
+    def begin(i, carry):
+        bring(i).start()
+        return carry
+
+    lax.fori_loop(0, pairs, begin, 0)
+    zero[...] = jnp.zeros(zero.shape, zero.dtype)
+    for block in range(blocks):
+        used[block] = 0
+
+    def pick(u, carry):
+        rows32[pl.ds(u, 1), :] = state_in[user_pos[u], 0:1, :]
+        return carry
+
+    lax.fori_loop(0, state.shape[0], pick, 0)
+    state[...] = rows32[...].astype(state.dtype)
 
     def one(i, carry):
         src = i // per_pair
         j = i - src * per_pair
         length = meta[src, 0, 4 * j + 1]
         offset = meta[src, 0, 4 * j + 2]
+        bring(i).wait()
         for b in range(MAXB):
-            fill = length - b * BLOCK
-
-            @pl.when(fill > 0)
-            def _():
-                value = arr[i, b * BLOCK : (b + 1) * BLOCK, :].astype(jnp.float32)
-                value = jnp.where(row < fill, value, 0.0).astype(packed.dtype)
-                packed[pl.ds(pl.multiple_of((offset + b) * BLOCK, BLOCK), BLOCK), :] = value
-
-        return carry
-
-    lax.fori_loop(0, dp_size * per_pair, one, 0)
-
-    def pick(u, carry):
-        pos = user_pos[u]
-        q = pos // slots
-        rows32[pl.ds(u, 1), :] = state_in[q, pl.ds(pos - q * slots, 1), :]
-        return carry
-
-    lax.fori_loop(0, state.shape[0], pick, 0)
-    state[...] = rows32[...].astype(state.dtype)
+
+            @pl.when(length > b * BLOCK)
+            def _():
+                used[offset + b] = 1
+                put(held.at[i, pl.ds(b * BLOCK, BLOCK)], offset + b).start()
+
+        return carry
+
+    lax.fori_loop(0, pairs, one, 0)
+
+    def fill(block, carry):
+        @pl.when(used[block] == 0)
+        def _():
+            put(zero, block).start()
+
+        return carry
+
+    lax.fori_loop(0, blocks, fill, 0)
+
+    def end(block, carry):
+        put(zero, block).wait()
+        return carry
+
+    lax.fori_loop(0, blocks, end, 0)
 
 
 def per_device(tokens, w_uvqk, w_out, hist_len, owner, recv_offset, block_start):
@@ -377,7 +412,6 @@
     pairs = dp_size * per_pair
     reach = dp_size // mp_size
     slots = reach * per_pair
-    slots_pad = -(-per_pair // 8) * 8
     quarter = D // mp_size
     rows = tokens.shape[0]
 
@@ -403,7 +437,7 @@
         out_shape=(
             jax.ShapeDtypeStruct((pairs, WIN, quarter), bf16),
             jax.ShapeDtypeStruct((dp_size, 1, 128), jnp.int32),
-            jax.ShapeDtypeStruct((dp_size, slots_pad, quarter), f32),
+            jax.ShapeDtypeStruct((pairs, 8, quarter), f32),
         ),
         in_specs=[anywhere, vmem, vmem, vmem],
         out_specs=(anywhere, anywhere, anywhere),
@@ -412,7 +446,7 @@
             pltpu.VMEM((mp_size, D, 4 * HEAD), bf16),
             pltpu.VMEM((D, D), bf16),
             pltpu.VMEM((slots, mp_size, WIN, quarter), bf16),
-            pltpu.VMEM((reach, mp_size, slots_pad, quarter), f32),
+            pltpu.VMEM((slots, mp_size, 8, quarter), f32),
             pltpu.VMEM((dp_size, 1, 128), jnp.int32),
             dma,
             dma((3,)),
@@ -423,26 +457,35 @@
             dma((slots,)),
             dma((slots, mp_size)),
             dma((pairs,)),
-            dma((reach * mp_size,)),
-            dma((dp_size,)),
+            dma((slots, mp_size)),
+            dma((pairs,)),
             dma,
         ],
         compiler_params=pltpu.CompilerParams(
-            collective_id=0, has_side_effects=True, vmem_limit_bytes=40 * 1024 * 1024
+            collective_id=0, has_side_effects=True, vmem_limit_bytes=60 * 1024 * 1024
         ),
         name="layer",
     )(picked, w_uvqk, w_out, meta)
-    return pl.pallas_call(
+    packed, state = pl.pallas_call(
         functools.partial(place_kernel, dp_size, per_pair),
         out_shape=(
-            jax.ShapeDtypeStruct((rows, quarter), bf16),
+            jax.ShapeDtypeStruct((rows // BLOCK, BLOCK, quarter), bf16),
             jax.ShapeDtypeStruct((user_count, quarter), bf16),
         ),
-        in_specs=[smem, smem, vmem, vmem],
-        out_specs=(vmem, vmem),
-        scratch_shapes=[pltpu.VMEM((user_count, quarter), f32)],
+        in_specs=[smem, smem, anywhere, vmem],
+        out_specs=(anywhere, vmem),
+        scratch_shapes=[
+            pltpu.VMEM((pairs, WIN, quarter), bf16),
+            pltpu.VMEM((BLOCK, quarter), bf16),
+            pltpu.VMEM((user_count, quarter), f32),
+            pltpu.SMEM((rows // BLOCK,), jnp.int32),
+            dma((pairs,)),
+            dma((rows // BLOCK,)),
+        ],
+        compiler_params=pltpu.CompilerParams(vmem_limit_bytes=60 * 1024 * 1024),
         name="place",
     )(meta_in, user_pos, arr, state_in)
+    return packed.reshape(rows, quarter), state
 
 
 def solution(mesh):

time: 79.8 us -> 67 us (0.84)
  Pallas kernels: 74.2 us -> 66 us
  local copies, waits for them, and re-layouts: 4.43 us -> 0 us
    pallas_call x1, Pallas kernels: 65.9 us -> 57.7 us  [per_device(): pl.pallas_call(functools.partial(layer_kernel, dp_size, mp_size, per_pair...]
    unnamed x14 -> x0, local copies, waits for them, and re-layouts: 4.43 us -> none
where the time goes in v3:
time: 67 us; the launch traced here: 66.6 us
  Pallas kernels  66 us (99%)
    pallas_call x1, Pallas kernels, per_device(): pl.pallas_call(functools.partial(layer_kernel, dp_size, mp_size, per_pair...  57.7 us
    pallas_call x1, Pallas kernels, per_device(): pl.pallas_call(functools.partial(place_kernel, dp_size, per_pair), out_sh...  4.33 us
    pallas_call x1, Pallas kernels, per_device(): pl.pallas_call(functools.partial(gather_kernel, dp_size, mp_size, per_pai...  3.96 us

profile of v3, /device:TPU:0, one launch (start us, length us, event | category | flops | bytes accessed | tf_op | source)
XLA Modules:
  0.0 66.6 jit_solution(4730485001461393907)
XLA Ops:
  0.6 4.0 %gather.1 = (s32[8,1,128]{2,1,0:T(1,128)}, s32[24]{0:T(128)}, bf16[6,2,128,512]{3,2,1,0:T(8,128)(2,1)}) custom-call(s32[1,24]{1,0:T(1,128)} %owner.1, s32[1,24]{1,0:T(1,128)} %hist_len.1, s32[1,24]{1,0:T(1,128)} %recv_offset.1, s32[1,24]{1,0:T(1,128)} %block_start.1, bf16[48,128,512]{2,1,0:T(8,128)(2,1)} %bitcast.2), custom_call_target="tpu_custom_call" | custom-call | tf_op jit(solution)/shard_map/gather/pallas_call | solution.py:423
  4.6 57.7 %layer.1 = (bf16[24,256,128]{2,1,0:T(8,128)(2,1)}, s32[8,1,128]{2,1,0:T(1,128)}, f32[24,8,128]{2,1,0:T(8,128)}) custom-call(bf16[6,2,128,512]{3,2,1,0:T(8,128)(2,1)} %get-tuple-element.10.rows_ref, bf16[512,512]{1,0:T(8,128)(2,1)} %w_ref.1, bf16[512,512]{1,0:T(8,128)(2,1)} %wout_ref.1, s32[8,1,128]{2,1,0:T(1,128)} %get-tuple-element.11.meta_ref), custom_call_target="tpu_custom_call" | custom-call | tf_op jit(solution)/shard_map/layer/pallas_call | solution.py:435
  62.3 4.3 %place.1 = (bf16[48,128,128]{2,1,0:T(8,128)(2,1)}, bf16[24,128]{1,0:T(8,128)(2,1)}) custom-call(s32[8,1,128]{2,1,0:T(1,128)} %get-tuple-element.12.meta, s32[24]{0:T(128)} %get-tuple-element.13.user_pos, bf16[24,256,128]{2,1,0:T(8,128)(2,1)} %get-tuple-element.14.arr, f32[24,8,128]{2,1,0:T(8,128)} %get-tuple-element.15.state_in), custom_call_target="tpu_custom_call" | custom-call | tf_op jit(solution)/shard_map/place/pallas_call | solution.py:469

commit v4 on v3

--- a/solution.py
+++ b/solution.py
@@ -138,7 +138,7 @@
 
     def travels(s):
         k = s // per_pair
-        return lax.rem(s - k * per_pair + k, 2) == 0
+        return s - k * per_pair == 0
 
     def start_rows(s, carry):
         away = jnp.logical_and(travels(s), target(s) != d)
@@ -299,6 +299,7 @@
     def turn(i, carry):
         late = i // slots
         s = i - late * slots
+        s = jnp.where(late == 0, slots - 1 - s, s)
 
         @pl.when(travels(s) == (late == 1))
         def _():

time: 67 us -> 63.4 us (0.946)
  Pallas kernels: 66 us -> 62.4 us
    pallas_call x1, Pallas kernels: 57.7 us -> 54.1 us  [per_device(): pl.pallas_call(functools.partial(layer_kernel, dp_size, mp_size, per_pair...]
where the time goes in v4:
time: 63.4 us; the launch traced here: 63.1 us
  Pallas kernels  62.4 us (98%)
  between operations  0.65 us (1%)
    pallas_call x1, Pallas kernels, per_device(): pl.pallas_call(functools.partial(layer_kernel, dp_size, mp_size, per_pair...  54.1 us
    pallas_call x1, Pallas kernels, per_device(): pl.pallas_call(functools.partial(place_kernel, dp_size, per_pair), out_sh...  4.37 us
    pallas_call x1, Pallas kernels, per_device(): pl.pallas_call(functools.partial(gather_kernel, dp_size, mp_size, per_pai...  3.96 us

profile of v4, /device:TPU:0, one launch (start us, length us, event | category | flops | bytes accessed | tf_op | source)
XLA Modules:
  0.0 63.1 jit_solution(14895935764784439692)
XLA Ops:
  0.6 4.0 %gather.1 = (s32[8,1,128]{2,1,0:T(1,128)}, s32[24]{0:T(128)}, bf16[6,2,128,512]{3,2,1,0:T(8,128)(2,1)}) custom-call(s32[1,24]{1,0:T(1,128)} %owner.1, s32[1,24]{1,0:T(1,128)} %hist_len.1, s32[1,24]{1,0:T(1,128)} %recv_offset.1, s32[1,24]{1,0:T(1,128)} %block_start.1, bf16[48,128,512]{2,1,0:T(8,128)(2,1)} %bitcast.2), custom_call_target="tpu_custom_call" | custom-call | tf_op jit(solution)/shard_map/gather/pallas_call | solution.py:424
  4.6 54.1 %layer.1 = (bf16[24,256,128]{2,1,0:T(8,128)(2,1)}, s32[8,1,128]{2,1,0:T(1,128)}, f32[24,8,128]{2,1,0:T(8,128)}) custom-call(bf16[6,2,128,512]{3,2,1,0:T(8,128)(2,1)} %get-tuple-element.10.rows_ref, bf16[512,512]{1,0:T(8,128)(2,1)} %w_ref.1, bf16[512,512]{1,0:T(8,128)(2,1)} %wout_ref.1, s32[8,1,128]{2,1,0:T(1,128)} %get-tuple-element.11.meta_ref), custom_call_target="tpu_custom_call" | custom-call | tf_op jit(solution)/shard_map/layer/pallas_call | solution.py:436
  58.7 4.4 %place.1 = (bf16[48,128,128]{2,1,0:T(8,128)(2,1)}, bf16[24,128]{1,0:T(8,128)(2,1)}) custom-call(s32[8,1,128]{2,1,0:T(1,128)} %get-tuple-element.12.meta, s32[24]{0:T(128)} %get-tuple-element.13.user_pos, bf16[24,256,128]{2,1,0:T(8,128)(2,1)} %get-tuple-element.14.arr, f32[24,8,128]{2,1,0:T(8,128)} %get-tuple-element.15.state_in), custom_call_target="tpu_custom_call" | custom-call | tf_op jit(solution)/shard_map/place/pallas_call | solution.py:470
